TPU v7x, 512 devices: a whole 4x4x16 slice. The times are simulated.
512 devices in a mesh: row: 32 (over y, x, core), col: 16 (over z).
Axes of the slice: x: 4, y: 4, z: 16, core: 2. Of those that a mesh axis runs over, the one named last changes fastest.
Arguments:
- positions: float32 [3, 262144], P(None, ('row', 'col')), may hold values from -6 to 6
- velocities: float32 [3, 262144], P(None, ('row', 'col')), may hold values from -6 to 6
- accels: float32 [3, 262144], P(None, ('row', 'col')), may hold values from -0.75 to 0.75
- jerks: float32 [3, 262144], P(None, ('row', 'col')), may hold values from -1.5 to 1.5
- masses: float32 [262144], P(('row', 'col')), may hold values from 0.3 to 3
- elapsed: float32 [262144], P(('row', 'col')), may hold values from 0.05 to 0.5
- active_star: int32 [4096], replicated, may hold values from 0 to 262143, as said below
Outputs:
- new_positions: float32 [3, 262144], P(None, ('row', 'col'))
- new_velocities: float32 [3, 262144], P(None, ('row', 'col'))
- new_accels: float32 [3, 262144], P(None, ('row', 'col'))
- new_jerks: float32 [3, 262144], P(None, ('row', 'col'))
Inputs may be any that keep to these rules, and one draw needn't show every extreme that they name: `active_star`: the 4096 ids are distinct. Star g is owned by device g // 512, devices counted with row slowest and col fastest. In each aligned block of 128 entries (one group of targets), at most 12 entries name stars whose owning device has the same col index, and in every block some col index has exactly 12.
All inputs are finite; a program needn't handle non-finite values.
Results may differ from a plain program's by a relative error of at most 0.0003.
Values sent between devices are 32-bit elements; how exact they have to be, the bound alone decides.
A program may use at most 64 MiB of HBM per device.

v0:
```python
import math

import jax
import jax.numpy as jnp
from jax import lax
from jax.sharding import PartitionSpec as P

softening = 0.001


def joined_along(tiles, dim):
    tiles = jnp.moveaxis(tiles, 0, dim)
    dims = tiles.shape
    return tiles.reshape(*dims[:dim], dims[dim] * dims[dim + 1], *dims[dim + 2 :])


def copy_for_each(array, axis):
    peers = lax.axis_size(axis)
    return lax.all_to_all(
        jnp.broadcast_to(array[None], (peers, *array.shape)), axis, 0, 0, tiled=True
    )


def gathered_copies(array, axis, dim):
    return joined_along(copy_for_each(array, axis), dim)


def of_everyone(array, axis):
    everything = copy_for_each(array, axis)
    return jnp.sum(everything, axis=0)


def predict(positions, velocities, accels, jerks, elapsed):
    timestep = elapsed[None, :]
    moved_pos = positions + timestep * (
        velocities + timestep * (0.5 * accels + timestep * jerks / 6.0)
    )
    moved_vel = velocities + timestep * (accels + 0.5 * timestep * jerks)
    return (moved_pos, moved_vel)


def correct(old_pos, old_vel, old_acc, old_jerk, new_acc, new_jerk, timestep):
    halfstep = 0.5 * timestep
    twelfth = timestep * timestep / 12.0
    new_vel = old_vel + halfstep * (old_acc + new_acc) + twelfth * (old_jerk - new_jerk)
    new_pos = old_pos + halfstep * (old_vel + new_vel) + twelfth * (old_acc - new_acc)
    return (new_pos, new_vel)


def pair_sums(targets, sources, ceiling):
    jcount = sources.shape[1]
    blk_width = math.gcd(jcount, ceiling)
    jpieces = jnp.transpose(sources.reshape(7, jcount // blk_width, blk_width), (1, 0, 2))

    def advance(running, jpiece):
        separation = jpiece[0:3, None, :] - targets[0:3, :, None]
        rel_velocity = jpiece[3:6, None, :] - targets[3:6, :, None]
        radius_sq = jnp.sum(separation * separation, axis=0) + softening
        inverse = lax.rsqrt(radius_sq)
        weight = jpiece[6][None, :] * inverse * inverse * inverse
        closing = 3.0 * jnp.sum(separation * rel_velocity, axis=0) / radius_sq
        accel_sum = jnp.sum(weight[None] * separation, axis=2)
        change = jnp.sum(weight[None] * (rel_velocity - closing[None] * separation), axis=2)
        return (running + jnp.concatenate([accel_sum, change], axis=0), None)

    initial = jnp.zeros((6, targets.shape[1]), jnp.float32)
    summed, unused = lax.scan(advance, initial, jpieces)
    return summed


def on_device(positions, velocities, accels, jerks, masses, elapsed, active_star):
    star_dev = positions.shape[1]
    row_count = lax.axis_size("row")
    col_count = lax.axis_size("col")
    row_index = lax.axis_index("row")
    col_index = lax.axis_index("col")
    device_id = row_index * col_count + col_index
    active_count = active_star.shape[0]
    group_size = active_count // row_count
    scale = 1.0 / (star_dev * row_count * col_count)
    highest = lax.Precision.HIGHEST
    moved_pos, moved_vel = predict(positions, velocities, accels, jerks, elapsed)
    sources = jnp.concatenate([moved_pos, moved_vel, masses[None, :]], axis=0)
    group_ids = lax.dynamic_slice_in_dim(active_star, row_index * group_size, group_size)
    in_column = group_ids // star_dev % col_count == col_index
    column_block = gathered_copies(sources, "row", 1)
    position_in = group_ids // star_dev // col_count * star_dev + group_ids % star_dev
    slot_rows = lax.broadcasted_iota(jnp.int32, (column_block.shape[1], group_size), 0)
    picker = ((slot_rows == position_in[None, :]) & in_column[None, :]).astype(jnp.float32)
    own_part = jnp.dot(
        column_block[0:6], picker, precision=highest, preferred_element_type=jnp.float32
    )
    targets = of_everyone(own_part, "col")
    partial_sums = pair_sums(targets, column_block, 512)
    forces = of_everyone(partial_sums, "col") * scale
    every_force = gathered_copies(forces, "row", 1)
    slot_cols = lax.broadcasted_iota(jnp.int32, (active_count, star_dev), 1)
    mine = (active_star // star_dev == device_id)[:, None]
    placer = (mine & ((active_star % star_dev)[:, None] == slot_cols)).astype(jnp.float32)
    landed = jnp.dot(every_force, placer, precision=highest, preferred_element_type=jnp.float32)
    flags = jnp.sum(placer, axis=0)
    active = (flags > 0.5)[None, :]
    new_acc = landed[0:3]
    new_jerk = landed[3:6]
    new_pos, new_vel = correct(
        positions, velocities, accels, jerks, new_acc, new_jerk, elapsed[None, :]
    )
    return (
        jnp.where(active, new_pos, positions),
        jnp.where(active, new_vel, velocities),
        jnp.where(active, new_acc, accels),
        jnp.where(active, new_jerk, jerks),
    )


def solution(mesh):
    placed = (
        P(None, ("row", "col")),
        P(None, ("row", "col")),
        P(None, ("row", "col")),
        P(None, ("row", "col")),
        P(("row", "col")),
        P(("row", "col")),
        P(),
    )
    return jax.shard_map(
        on_device,
        mesh=mesh,
        in_specs=placed,
        out_specs=(
            P(None, ("row", "col")),
            P(None, ("row", "col")),
            P(None, ("row", "col")),
            P(None, ("row", "col")),
        ),
        check_vma=False,
    )
```

profile of v0, /device:TPU:1, one launch (start us, length us, event | category | flops | bytes accessed | tf_op | source)
XLA Modules:
  0.0 114.2 jit_solution(2002937468598850159)
XLA Ops:
  0.6 0.7 multiply_multiply_fusion.1
  1.3 0.8 multiply_add_fusion.2
  2.1 0.7 pad_maximum_fusion
  2.8 0.9 broadcast_in_dim.36
  3.6 10.5 %all-to-all-start = ((f32[32,7,512]{2,1,0:T(8,128)}), f32[32,7,512]{2,1,0:T(8,128)S(1)}, u32[]{:S(2)}, u32[]{:S(2)}) async-start(f32[32,7,512]{2,1,0:T(8,128)} %broadcast_in_dim.36), calls=%async_computation | async-start | bytes 1048576 | tf_op jit(solution)/shard_map/all_to_all | solution.py:19
  14.4 11.3 %all-to-all-done = f32[32,7,512]{2,1,0:T(8,128)S(1)} async-done(((f32[32,7,512]{2,1,0:T(8,128)}), f32[32,7,512]{2,1,0:T(8,128)S(1)}, u32[]{:S(2)}, u32[]{:S(2)}) %all-to-all-start) | async-done | bytes 458784 | tf_op jit(solution)/shard_map/all_to_all | solution.py:19
  25.7 3.0 %fusion.9 = f32[6,128]{1,0:T(8,128)S(1)} fusion(f32[6,16384]{1,0:T(8,128)S(1)} %bitcast.19, s32[128]{0:T(128)S(1)} %fusion.19, pred[128]{0:T(512)(128)(4,1)S(1)} %get-tuple-element.54), kind=kOutput, calls=%fused_computation.22 | convolution fusion | flops 155189248 | bytes 396928 | tf_op jit(solution)/shard_map/dot_general | solution.py:90
  28.7 0.6 broadcast_in_dim.37
  29.4 13.0 %all-to-all-start.1 = ((f32[16,6,128]{2,1,0:T(8,128)}), f32[16,6,128]{2,1,0:T(8,128)S(1)}, u32[]{:S(2)}, u32[]{:S(2)}) async-start(f32[16,6,128]{2,1,0:T(8,128)} %broadcast_in_dim.37), calls=%async_computation.1 | async-start | bytes 131072 | tf_op jit(solution)/shard_map/all_to_all | solution.py:19
  42.4 11.6 %all-to-all-done.1 = f32[16,6,128]{2,1,0:T(8,128)S(1)} async-done(((f32[16,6,128]{2,1,0:T(8,128)}), f32[16,6,128]{2,1,0:T(8,128)S(1)}, u32[]{:S(2)}, u32[]{:S(2)}) %all-to-all-start.1) | async-done | bytes 49184 | tf_op jit(solution)/shard_map/all_to_all | solution.py:19
  54.0 25.5 %while.11 = (s32[]{:T(128)}, f32[6,128]{1,0:T(8,128)S(1)}, f32[32,7,512]{2,1,0:T(8,128)S(1)}, f32[6,128]{1,0:T(8,128)S(1)}, s32[]{:T(128)}, /*index=5*/s32[]{:T(128)}, s32[]{}, s32[]{}) while((s32[]{:T(128)}, f32[6,128]{1,0:T(8,128)S(1)}, f32[32,7,512]{2,1,0:T(8,128)S(1)}, f32[6,128]{1,0:T(8,128)S(1)}, s32[]{:T(128)}, ...), condition=%wide.region_7.8_spmd.clone, body=%wide.region_2.0_spmd.clone.sunk | while | flops 3016197 | bytes 2177159 | solution.py:67
  54.4 0.4 fusion.28
  55.2 0.4 fusion.28
  56.0 0.4 fusion.28
  56.8 0.4 fusion.28
  57.6 0.4 fusion.28
  58.4 0.4 fusion.28
  59.2 0.4 fusion.28
  60.0 0.4 fusion.28
  60.8 0.4 fusion.28
  61.6 0.4 fusion.28
  62.3 0.4 fusion.28
  63.9 0.4 fusion.28
  64.7 0.4 fusion.28
  65.5 0.4 fusion.28
  66.3 0.4 fusion.28
  67.1 0.4 fusion.28
  67.9 0.4 fusion.28
  68.7 0.4 fusion.28
  69.5 0.4 fusion.28
  70.3 0.4 fusion.28
  71.1 0.4 fusion.28
  71.9 0.4 fusion.28
  72.7 0.4 fusion.28
  73.5 0.4 fusion.28
  74.3 0.4 fusion.28
  75.1 0.4 fusion.28
  75.9 0.4 fusion.28
  76.7 0.4 fusion.28
  79.5 0.6 broadcast_in_dim.38
  80.2 4.0 %all-to-all-start.2 = ((f32[16,6,128]{2,1,0:T(8,128)}), f32[16,6,128]{2,1,0:T(8,128)S(1)}, u32[]{:S(2)}, u32[]{:S(2)}) async-start(f32[16,6,128]{2,1,0:T(8,128)} %broadcast_in_dim.38), calls=%async_computation.2 | async-start | bytes 131072 | tf_op jit(solution)/shard_map/all_to_all | solution.py:19
  84.1 2.8 %convert_reduce_fusion = f32[512]{0:T(512)S(1)} fusion(s32[4096]{0:T(1024)S(1)} %add_select_fusion, pred[4096]{0:T(1024)(128)(4,1)S(1)} %fusion.16), kind=kLoop, calls=%fused_computation.17 | loop fusion | flops 8388096 | bytes 22528 | tf_op jit(solution)/shard_map/reduce_sum | solution.py:101
  86.9 8.8 %all-to-all-done.2 = f32[16,6,128]{2,1,0:T(8,128)S(1)} async-done(((f32[16,6,128]{2,1,0:T(8,128)}), f32[16,6,128]{2,1,0:T(8,128)S(1)}, u32[]{:S(2)}, u32[]{:S(2)}) %all-to-all-start.2) | async-done | bytes 49184 | tf_op jit(solution)/shard_map/all_to_all | solution.py:19
  95.7 0.7 broadcast_in_dim.39
  96.4 6.4 %all-to-all-start.3 = ((f32[32,6,128]{2,1,0:T(8,128)}), f32[32,6,128]{2,1,0:T(8,128)S(1)}, u32[]{:S(2)}, u32[]{:S(2)}) async-start(f32[32,6,128]{2,1,0:T(8,128)} %broadcast_in_dim.39), calls=%async_computation.3 | async-start | bytes 262144 | tf_op jit(solution)/shard_map/all_to_all | solution.py:19
  102.9 7.7 %all-to-all-done.3 = f32[32,6,128]{2,1,0:T(8,128)S(1)} async-done(((f32[32,6,128]{2,1,0:T(8,128)}), f32[32,6,128]{2,1,0:T(8,128)S(1)}, u32[]{:S(2)}, u32[]{:S(2)}) %all-to-all-start.3) | async-done | bytes 98336 | tf_op jit(solution)/shard_map/all_to_all | solution.py:19
  110.5 3.0 %fusion.6 = f32[6,512]{1,0:T(8,128)S(1)} fusion(s32[4096]{0:T(1024)S(1)} %add_select_fusion, pred[4096]{0:T(1024)(128)(4,1)S(1)} %fusion.16, f32[32,6,128]{2,1,0:T(8,128)S(1)} %all-to-all-done.3), kind=kOutput, calls=%fused_computation.20 | convolution fusion | flops 155189248 | bytes 131072 | tf_op jit(solution)/shard_map/dot_general | solution.py:100
  113.5 0.6 broadcast_select_fusion
  (215 shorter events, 12.7 us)
Async XLA Ops:
  3.6 10.5 %copy-start = (s32[4096]{0:T(1024)S(1)}, s32[4096]{0:T(1024)}, u32[]{:S(2)}) copy-start(s32[4096]{0:T(1024)} %param.15) | copy-start | bytes 49156
  3.6 22.1 %all-to-all-start = ((f32[32,7,512]{2,1,0:T(8,128)}), f32[32,7,512]{2,1,0:T(8,128)S(1)}, u32[]{:S(2)}, u32[]{:S(2)}) async-start(f32[32,7,512]{2,1,0:T(8,128)} %broadcast_in_dim.36), calls=%async_computation | async-start | bytes 1048576 | tf_op jit(solution)/shard_map/all_to_all | solution.py:19
  29.4 24.6 %all-to-all-start.1 = ((f32[16,6,128]{2,1,0:T(8,128)}), f32[16,6,128]{2,1,0:T(8,128)S(1)}, u32[]{:S(2)}, u32[]{:S(2)}) async-start(f32[16,6,128]{2,1,0:T(8,128)} %broadcast_in_dim.37), calls=%async_computation.1 | async-start | bytes 131072 | tf_op jit(solution)/shard_map/all_to_all | solution.py:19
  80.2 15.5 %all-to-all-start.2 = ((f32[16,6,128]{2,1,0:T(8,128)}), f32[16,6,128]{2,1,0:T(8,128)S(1)}, u32[]{:S(2)}, u32[]{:S(2)}) async-start(f32[16,6,128]{2,1,0:T(8,128)} %broadcast_in_dim.38), calls=%async_computation.2 | async-start | bytes 131072 | tf_op jit(solution)/shard_map/all_to_all | solution.py:19
  96.4 14.2 %all-to-all-start.3 = ((f32[32,6,128]{2,1,0:T(8,128)}), f32[32,6,128]{2,1,0:T(8,128)S(1)}, u32[]{:S(2)}, u32[]{:S(2)}) async-start(f32[32,6,128]{2,1,0:T(8,128)} %broadcast_in_dim.39), calls=%async_computation.3 | async-start | bytes 262144 | tf_op jit(solution)/shard_map/all_to_all | solution.py:19
  102.8 10.7 %copy-start.1 = (f32[3,512]{1,0:T(4,128)S(1)}, f32[3,512]{1,0:T(4,128)}, u32[]{:S(2)}) copy-start(f32[3,512]{1,0:T(4,128)} %param.10) | copy-start | bytes 18436
  102.8 10.7 %copy-start.2 = (f32[3,512]{1,0:T(4,128)S(1)}, f32[3,512]{1,0:T(4,128)}, u32[]{:S(2)}) copy-start(f32[3,512]{1,0:T(4,128)} %param.12) | copy-start | bytes 18436
  102.9 10.7 %copy-start.3 = (f32[3,512]{1,0:T(4,128)S(1)}, f32[3,512]{1,0:T(4,128)}, u32[]{:S(2)}) copy-start(f32[3,512]{1,0:T(4,128)} %param.9) | copy-start | bytes 18436
  102.9 10.7 %copy-start.4 = (f32[3,512]{1,0:T(4,128)S(1)}, f32[3,512]{1,0:T(4,128)}, u32[]{:S(2)}) copy-start(f32[3,512]{1,0:T(4,128)} %param.11) | copy-start | bytes 18436
where the time goes:
time: 115 us; the launch traced here: 114 us
  waiting for transfers between devices  39.3 us (34%)
  starting transfers between devices  33.9 us (29%)
  other arithmetic  28.5 us (25%)
  matrix products  6 us (5%)
  local copies, waits for them, and re-layouts  3.72 us (3%)
  loops' own time  1.93 us (2%)
    all_to_all x4, waiting for transfers between devices, copy_for_each(): lax.all_to_all(jnp.broadcast_to(array[None], (peers, *array.shape)), axis...  39.3 us
    all_to_all x4, starting transfers between devices, copy_for_each(): lax.all_to_all(jnp.broadcast_to(array[None], (peers, *array.shape)), axis...  33.9 us
    reduce_sum x32, other arithmetic, advance(): accel_sum = jnp.sum(weight[None] * separation, axis=2)  12.9 us
    reduce_sum x32, other arithmetic, advance(): radius_sq = jnp.sum(separation * separation, axis=0) + softening  6.91 us
    dot_general x1, matrix products, on_device(): jnp.dot(column_block[0:6], picker, precision=highest, preferred_element_t...  3.04 us
    dot_general x1, matrix products, on_device(): jnp.dot(every_force, placer, precision=highest, preferred_element_type=jn...  2.96 us
    reduce_sum x1, other arithmetic, on_device(): flags = jnp.sum(placer, axis=0)  2.81 us
    broadcast_in_dim x4, local copies, waits for them, and re-layouts, copy_for_each(): jnp.broadcast_to(array[None], (peers, *array.shape))  2.77 us
  transfers between devices with their start and end apart: 4, of which 4 were waited for; matrix products, arithmetic and copies ran while one was open for 3% of the time, Pallas kernels for 0%

commit v1 on v0

v1 whole, which is shorter than its diff:
```python
import functools

import jax
import jax.numpy as jnp
from jax import lax
from jax.experimental import pallas as pl
from jax.experimental.pallas import tpu as pltpu
from jax.sharding import PartitionSpec as P

softening = 0.001
LANES = 128
MESH = pl.DeviceIdType.MESH


def correct(old_pos, old_vel, old_acc, old_jerk, new_acc, new_jerk, timestep):
    halfstep = 0.5 * timestep
    twelfth = timestep * timestep / 12.0
    new_vel = old_vel + halfstep * (old_acc + new_acc) + twelfth * (old_jerk - new_jerk)
    new_pos = old_pos + halfstep * (old_vel + new_vel) + twelfth * (old_acc - new_acc)
    return (new_pos, new_vel)


def split_moments(block):
    rows = lax.broadcasted_iota(jnp.int32, block.shape, 0)
    weighted = block * jnp.where(rows < 6, block[6:7], 1.0)
    high = weighted.astype(jnp.bfloat16).astype(jnp.float32)
    rest = weighted - high
    middle = rest.astype(jnp.bfloat16).astype(jnp.float32)
    low = rest - middle
    return jnp.concatenate([high, middle, low, jnp.zeros_like(block)], axis=0).astype(jnp.bfloat16)


def weigh_block(srcs, block, tb, wbuf, bbuf, rbuf, slot):
    width = srcs.shape[2]
    moments = split_moments(srcs[block])
    rbuf[slot, :, 0:width] = moments
    rbuf[slot, :, width : 2 * width] = moments
    for chunk in range(width // LANES):
        lanes = pl.ds(chunk * LANES, LANES)
        high = pl.ds(chunk * LANES, LANES)
        low = pl.ds(width + chunk * LANES, LANES)
        source = [
            jnp.broadcast_to(srcs[block, k : k + 1, lanes], (16, LANES)) for k in range(6)
        ]
        for part in range(tb.shape[1] // 16):
            rows = pl.ds(part * 16, 16)
            dx, dy, dz, ux, uy, uz = [source[k] - tb[k, rows, :] for k in range(6)]
            radius_sq = (dx * dx + dy * dy) + (dz * dz + softening)
            inverse = lax.rsqrt(radius_sq)
            inverse_sq = inverse * inverse
            weight = inverse * inverse_sq
            closing = (dx * ux + dy * uy) + dz * uz
            bend = (weight * inverse_sq) * closing
            weight_high = weight.astype(jnp.bfloat16)
            bend_high = bend.astype(jnp.bfloat16)
            wbuf[slot, rows, high] = weight_high
            wbuf[slot, rows, low] = (weight - weight_high.astype(jnp.float32)).astype(jnp.bfloat16)
            bbuf[slot, rows, high] = bend_high
            bbuf[slot, rows, low] = (bend - bend_high.astype(jnp.float32)).astype(jnp.bfloat16)


def add_block(wbuf, bbuf, rbuf, wacc, bacc, slot):
    dims = (((1,), (1,)), ((), ()))
    moments = rbuf[slot]
    wacc[...] += lax.dot_general(wbuf[slot], moments, dims, preferred_element_type=jnp.float32)
    bacc[...] += lax.dot_general(bbuf[slot], moments, dims, preferred_element_type=jnp.float32)


def spread_targets(targets, tb):
    count = targets.shape[1]
    square = jnp.concatenate([targets] * (count // 8), axis=0)
    columns = square.T
    for k in range(6):
        tb[k] = jnp.broadcast_to(columns[:, k : k + 1], (count, LANES))


def pair_sums(srcs, targets, tb, wbuf, bbuf, rbuf, wacc, bacc):
    blocks = srcs.shape[0]
    spread_targets(targets, tb)
    wacc[...] = jnp.zeros_like(wacc)
    bacc[...] = jnp.zeros_like(bacc)
    wbuf[1] = jnp.zeros(wbuf.shape[1:], wbuf.dtype)
    bbuf[1] = jnp.zeros(bbuf.shape[1:], bbuf.dtype)
    rbuf[1] = jnp.zeros(rbuf.shape[1:], rbuf.dtype)

    def advance(j, carry):
        weigh_block(srcs, 2 * j, tb, wbuf, bbuf, rbuf, 0)
        add_block(wbuf, bbuf, rbuf, wacc, bacc, 1)
        weigh_block(srcs, 2 * j + 1, tb, wbuf, bbuf, rbuf, 1)
        add_block(wbuf, bbuf, rbuf, wacc, bacc, 0)
        return carry

    lax.fori_loop(0, blocks // 2, advance, 0)
    add_block(wbuf, bbuf, rbuf, wacc, bacc, 1)

    def folded(total):
        padded = jnp.concatenate([total, jnp.zeros((total.shape[0], LANES - 32), jnp.float32)], axis=1)
        turned = padded.T
        moment = turned[0:8] + turned[8:16] + turned[16:24]
        return moment - targets * moment[6:7]

    direct = folded(wacc[...])
    bent = folded(bacc[...])
    rows = lax.broadcasted_iota(jnp.int32, direct.shape, 0)
    shifted = pltpu.roll(bent, 3, 0)
    both = jnp.where(rows >= 3, direct - 3.0 * shifted, direct)
    return jnp.where(rows < 6, both, 0.0)


def take_lanes(tile, index):
    return jnp.take_along_axis(tile, index, axis=1, mode="promise_in_bounds")


def step_kernel(
    rows_n,
    cols_n,
    pos_h,
    vel_h,
    acc_h,
    jrk_h,
    mass_h,
    ela_h,
    ids_h,
    landed,
    pos,
    vel,
    acc,
    jrk,
    mass,
    ela,
    ids,
    srcs,
    picked,
    near,
    mine,
    far,
    part,
    parts,
    force,
    forces,
    found,
    tb,
    wbuf,
    bbuf,
    rbuf,
    wacc,
    bacc,
    in_sems,
    send_sems,
    recv_sems,
):
    row = lax.axis_index("row")
    col = lax.axis_index("col")
    stars = pos.shape[1]
    slots = stars // LANES
    groups = ids.shape[0]
    scale = 1.0 / (stars * rows_n * cols_n)

    loads = [
        pltpu.make_async_copy(src, dst, in_sems.at[i])
        for i, (src, dst) in enumerate(
            zip((pos_h, vel_h, acc_h, jrk_h, mass_h, ela_h, ids_h), (pos, vel, acc, jrk, mass, ela, ids))
        )
    ]
    for load in loads:
        load.start()

    barrier = pltpu.get_barrier_semaphore()
    for d in range(1, rows_n):
        pl.semaphore_signal(
            barrier, 1, device_id={"row": lax.rem(row + d, rows_n)}, device_id_type=MESH
        )
    for d in range(1, cols_n):
        pl.semaphore_signal(
            barrier, 1, device_id={"col": lax.rem(col + d, cols_n)}, device_id_type=MESH
        )

    for load in loads:
        load.wait()

    t = ela[...]
    p, v, a, j = pos[...], vel[...], acc[...], jrk[...]
    moved_pos = p + t * (v + t * (0.5 * a + t * j / 6.0))
    moved_vel = v + t * (a + 0.5 * t * j)
    own = rows_n - 1
    srcs[own] = jnp.concatenate(
        [moved_pos, moved_vel, mass[...], jnp.zeros((1, stars), jnp.float32)], axis=0
    )

    first = (row * cols_n + col) * stars

    def pick(g, carry):
        local = jnp.broadcast_to(ids[pl.ds(g, 1), :], (8, LANES)) - first
        inside = jnp.logical_and(local >= 0, local < stars)
        lane = jnp.bitwise_and(local, LANES - 1)
        tile = jnp.zeros((8, LANES), jnp.float32)
        for s in range(slots):
            held = jnp.logical_and(local >= s * LANES, local < (s + 1) * LANES)
            tile = jnp.where(held, take_lanes(srcs[own, :, s * LANES : (s + 1) * LANES], lane), tile)
        picked[g] = jnp.where(inside, tile, 0.0)
        return carry

    lax.fori_loop(0, groups, pick, 0, unroll=4)

    pl.semaphore_wait(barrier, rows_n - 1 + cols_n - 1)

    def send(src, dst, sem, axis, peer):
        copy = pltpu.make_async_remote_copy(
            src_ref=src,
            dst_ref=dst,
            send_sem=send_sems.at[sem],
            recv_sem=recv_sems.at[sem],
            device_id={axis: peer},
            device_id_type=MESH,
        )
        copy.start()

    def whole(ref, sem):
        return pltpu.make_async_remote_copy(
            src_ref=ref,
            dst_ref=ref,
            send_sem=send_sems.at[sem],
            recv_sem=recv_sems.at[sem],
            device_id={"row": row},
            device_id_type=MESH,
        )

    for d in range(1, rows_n):
        peer = lax.rem(row + d, rows_n)
        send(picked.at[peer], near.at[d - 1], 0, "row", peer)
    for d in range(1, rows_n):
        peer = lax.rem(row + d, rows_n)
        send(srcs.at[own], srcs.at[d - 1], 1, "row", peer)

    sublane = lax.broadcasted_iota(jnp.int32, (8, LANES), 0)
    lane_f = lax.broadcasted_iota(jnp.int32, (8, LANES), 1).astype(jnp.float32)

    def find(k, carry):
        star = first + k * 8 + sublane
        at = jnp.full((8, LANES), -1.0, jnp.float32)
        for g in range(groups):
            at = jnp.where(jnp.broadcast_to(ids[g : g + 1, :], (8, LANES)) == star, float(g), at)
        found[pl.ds(pl.multiple_of(k * 8, 8), 8), :] = jnp.where(at >= 0.0, at * LANES + lane_f, -1.0)
        return carry

    lax.fori_loop(0, stars // 8, find, 0, unroll=2)
    spots = [
        jnp.max(found[s * LANES : (s + 1) * LANES, :].T, axis=0, keepdims=True) for s in range(slots)
    ]

    whole(near, 0).wait_recv()
    total = picked[row]
    for d in range(rows_n - 1):
        total = total + near[d]
    mine[...] = total
    order = sorted(range(1, cols_n), key=lambda d: -min(d, cols_n - d))
    for d in order:
        send(mine, far.at[d - 1], 2, "col", lax.rem(col + d, cols_n))
    whole(far, 2).wait_recv()
    targets = mine[...]
    for d in range(cols_n - 1):
        targets = targets + far[d]

    whole(srcs.at[pl.ds(0, own)], 1).wait_recv()
    summed = pair_sums(srcs, targets, tb, wbuf, bbuf, rbuf, wacc, bacc)

    part[...] = summed
    for d in order:
        send(part, parts.at[d - 1], 3, "col", lax.rem(col + d, cols_n))
    whole(parts, 3).wait_recv()
    total = part[...]
    for d in range(cols_n - 1):
        total = total + parts[d]
    force[...] = total * scale
    for d in range(1, rows_n):
        send(force, forces.at[d - 1], 4, "row", lax.rem(row + d, rows_n))
    places = []
    for s in range(slots):
        spot = jnp.broadcast_to(spots[s], (8, LANES)).astype(jnp.int32)
        group = lax.shift_right_arithmetic(spot, 7)
        places.append((group, jnp.bitwise_and(spot, LANES - 1)))
    whole(forces, 4).wait_recv()

    top = lax.broadcasted_iota(jnp.int32, (8, LANES), 0)
    for s in range(slots):
        group, lane = places[s]
        out = jnp.where(group == row, take_lanes(force[...], lane), 0.0)
        for d in range(1, rows_n):
            sender = lax.rem(row + rows_n - d, rows_n)
            out = jnp.where(group == sender, take_lanes(forces[d - 1], lane), out)
        flag = jnp.where(group >= 0, 1.0, 0.0)
        landed[:, s * LANES : (s + 1) * LANES] = jnp.where(top == 6, flag, out)

    whole(near, 0).wait_send()
    whole(srcs.at[pl.ds(0, own)], 1).wait_send()
    whole(far, 2).wait_send()
    whole(parts, 3).wait_send()
    whole(forces, 4).wait_send()


def on_device(rows_n, cols_n, positions, velocities, accels, jerks, masses, elapsed, active_star):
    stars = positions.shape[1]
    groups = rows_n
    size = active_star.shape[0] // groups
    f32 = jnp.float32
    tile = (8, LANES)
    landed = pl.pallas_call(
        functools.partial(step_kernel, rows_n, cols_n),
        out_shape=jax.ShapeDtypeStruct((8, stars), f32),
        in_specs=[pl.BlockSpec(memory_space=pl.ANY)] * 7,
        out_specs=pl.BlockSpec(memory_space=pltpu.VMEM),
        scratch_shapes=[
            pltpu.VMEM((3, stars), f32),
            pltpu.VMEM((3, stars), f32),
            pltpu.VMEM((3, stars), f32),
            pltpu.VMEM((3, stars), f32),
            pltpu.VMEM((1, stars), f32),
            pltpu.VMEM((1, stars), f32),
            pltpu.VMEM((groups, size), jnp.int32),
            pltpu.VMEM((rows_n, 8, stars), f32),
            pltpu.VMEM((groups,) + tile, f32),
            pltpu.VMEM((rows_n - 1,) + tile, f32),
            pltpu.VMEM(tile, f32),
            pltpu.VMEM((cols_n - 1,) + tile, f32),
            pltpu.VMEM(tile, f32),
            pltpu.VMEM((cols_n - 1,) + tile, f32),
            pltpu.VMEM(tile, f32),
            pltpu.VMEM((rows_n - 1,) + tile, f32),
            pltpu.VMEM((stars, LANES), f32),
            pltpu.VMEM((6, size, LANES), f32),
            pltpu.VMEM((2, size, 2 * stars), jnp.bfloat16),
            pltpu.VMEM((2, size, 2 * stars), jnp.bfloat16),
            pltpu.VMEM((2, 32, 2 * stars), jnp.bfloat16),
            pltpu.VMEM((size, 32), f32),
            pltpu.VMEM((size, 32), f32),
            pltpu.SemaphoreType.DMA((7,)),
            pltpu.SemaphoreType.DMA((5,)),
            pltpu.SemaphoreType.DMA((5,)),
        ],
        compiler_params=pltpu.CompilerParams(collective_id=0, has_side_effects=True),
        name="block_step",
    )(
        positions,
        velocities,
        accels,
        jerks,
        masses[None, :],
        elapsed[None, :],
        active_star.reshape(groups, size),
    )
    active = landed[6:7] > 0.5
    new_acc = landed[0:3]
    new_jerk = landed[3:6]
    new_pos, new_vel = correct(
        positions, velocities, accels, jerks, new_acc, new_jerk, elapsed[None, :]
    )
    return (
        jnp.where(active, new_pos, positions),
        jnp.where(active, new_vel, velocities),
        jnp.where(active, new_acc, accels),
        jnp.where(active, new_jerk, jerks),
    )


def solution(mesh):
    split = P(None, ("row", "col"))
    flat = P(("row", "col"))
    return jax.shard_map(
        functools.partial(on_device, mesh.shape["row"], mesh.shape["col"]),
        mesh=mesh,
        in_specs=(split, split, split, split, flat, flat, P()),
        out_specs=(split, split, split, split),
        check_vma=False,
    )
```

time: 115 us -> 63.6 us (0.55)
  Pallas kernels: 0 us -> 59.6 us
  waiting for transfers between devices: 39.3 us -> 0 us
  starting transfers between devices: 33.9 us -> 0 us
  other arithmetic: 28.5 us -> 2.16 us
  matrix products: 6 us -> 0 us
  local copies, waits for them, and re-layouts: 3.72 us -> 0.69 us
  loops' own time: 1.93 us -> 0 us
    pallas_call x0 -> x1, Pallas kernels: none -> 59.6 us  [on_device(): pl.pallas_call(functools.partial(step_kernel, rows_n, cols_n), out_shape=...]
    all_to_all x4 -> x0, waiting for transfers between devices: 39.3 us -> none  [copy_for_each(): lax.all_to_all(jnp.broadcast_to(array[None], (peers, *array.shape)), axis...]
    all_to_all x4 -> x0, starting transfers between devices: 33.9 us -> none  [copy_for_each(): lax.all_to_all(jnp.broadcast_to(array[None], (peers, *array.shape)), axis...]
    reduce_sum x67 -> x0, other arithmetic: 22.6 us -> none  [the longest x32 12.9 us: advance(): accel_sum = jnp.sum(weight[None] * separation, axis=2)]
    dot_general x2 -> x0, matrix products: 6 us -> none  [the longest x1 3.04 us: on_device(): jnp.dot(column_block[0:6], picker, precision=highest, preferred_element_t...]
    div x33 -> x0, other arithmetic: 3.28 us -> none  [the longest x32 2.59 us: advance(): closing = 3.0 * jnp.sum(separation * rel_velocity, axis=0) / radius_sq]
    broadcast_in_dim x4 -> x0, local copies, waits for them, and re-layouts: 2.77 us -> none  [copy_for_each(): jnp.broadcast_to(array[None], (peers, *array.shape))]
    another operation x1 -> x0, loops' own time: 1.93 us -> none  [pair_sums(): summed, unused = lax.scan(advance, initial, jpieces)]
  transfers between devices with their start and end apart: 4 -> 0, of which waited for: 4 -> 0; matrix products, arithmetic and copies ran while one was open for 3% -> 0% of each run, Pallas kernels for 0% -> 0%
where the time goes in v1:
time: 63.6 us; the launch traced here: 63.1 us
  Pallas kernels  59.6 us (94%)
  other arithmetic  2.16 us (3%)
  local copies, waits for them, and re-layouts  0.69 us (1%)
  between operations  0.69 us (1%)
    pallas_call x1, Pallas kernels, on_device(): pl.pallas_call(functools.partial(step_kernel, rows_n, cols_n), out_shape=...  59.6 us
    select_n x1, other arithmetic, on_device(): jnp.where(active, new_vel, velocities)  1.42 us

profile of v1, /device:TPU:1, one launch (start us, length us, event | category | flops | bytes accessed | tf_op | source)
XLA Modules:
  0.0 63.1 jit_solution(8229455420244234799)
XLA Ops:
  0.6 0.0 copy-start.4
  0.6 0.7 %copy-done.4 = f32[512]{0:T(512)S(1)} copy-done((f32[512]{0:T(512)S(1)}, f32[512]{0:T(512)}, u32[]{:S(2)}) %copy-start.4) | copy-done | bytes 2072
  1.3 0.0 copy-start
  1.3 0.0 copy-start.1
  1.3 0.0 copy-start.2
  1.3 0.0 copy-start.3
  1.3 59.6 %block_step.1 = f32[8,512]{1,0:T(8,128)} custom-call(f32[3,512]{1,0:T(4,128)} %pos_h.1, f32[3,512]{1,0:T(4,128)} %vel_h.1, f32[3,512]{1,0:T(4,128)} %acc_h.1, f32[3,512]{1,0:T(4,128)} %jrk_h.1, f32[1,512]{1,0:T(1,128)} %bitcast.5, f32[1,512]{1,0:T(1,128)} %bitcast.4, s32[32,128]{1,0:T(8,128)} %bitcast.3), custom_call_target="tpu_custom_call" | custom-call | tf_op jit(solution)/shard_map/block_step/pallas_call | solution.py:307
  60.9 0.7 %compare_reduce_fusion = pred[512]{0:T(512)(128)(4,1)S(1)} fusion(f32[8,512]{1,0:T(8,128)} %block_step.1), kind=kLoop, calls=%fused_computation.2 | loop fusion | flops 512 | bytes 2560 | tf_op jit(solution)/shard_map/gt | solution.py:351
  61.7 0.0 copy-done
  61.7 0.0 copy-done.1
  61.7 0.0 copy-done.2
  61.7 0.0 copy-done.3
  61.7 1.4 %broadcast_select_fusion = (f32[3,512]{1,0:T(4,128)}, f32[3,512]{1,0:T(4,128)}, f32[3,512]{1,0:T(4,128)}, f32[3,512]{1,0:T(4,128)}) fusion(f32[3,512]{1,0:T(4,128)S(1)} %copy-done, pred[512]{0:T(512)(128)(4,1)S(1)} %compare_reduce_fusion, f32[3,512]{1,0:T(4,128)S(1)} %copy-done.3, f32[8,512]{1,0:T(8,128)} %block_step.1, f32[512]{0:T(512)S(1)} %get-tuple-element.9, ...), kind=kLoop, calls=%fused_computation.5 | loop fusion | flops 24576 | bytes 66048 | tf_op jit(solution)/shard_map/jit(_where)/select_n | solution.py:359
  (1 shorter events, 0.0 us)
Async XLA Ops:
  0.6 0.7 %copy-start.4 = (f32[512]{0:T(512)S(1)}, f32[512]{0:T(512)}, u32[]{:S(2)}) copy-start(f32[512]{0:T(512)} %param.12) | copy-start | bytes 6148
  1.3 60.4 %copy-start = (f32[3,512]{1,0:T(4,128)S(1)}, f32[3,512]{1,0:T(4,128)}, u32[]{:S(2)}) copy-start(f32[3,512]{1,0:T(4,128)} %vel_h.1) | copy-start | bytes 18436
  1.3 60.4 %copy-start.1 = (f32[3,512]{1,0:T(4,128)S(1)}, f32[3,512]{1,0:T(4,128)}, u32[]{:S(2)}) copy-start(f32[3,512]{1,0:T(4,128)} %pos_h.1) | copy-start | bytes 18436
  1.3 60.4 %copy-start.2 = (f32[3,512]{1,0:T(4,128)S(1)}, f32[3,512]{1,0:T(4,128)}, u32[]{:S(2)}) copy-start(f32[3,512]{1,0:T(4,128)} %acc_h.1) | copy-start | bytes 18436
  1.3 60.4 %copy-start.3 = (f32[3,512]{1,0:T(4,128)S(1)}, f32[3,512]{1,0:T(4,128)}, u32[]{:S(2)}) copy-start(f32[3,512]{1,0:T(4,128)} %jrk_h.1) | copy-start | bytes 18436

commit v2 on v1

v2 whole, which is shorter than its diff:
```python
import functools

import jax
import jax.numpy as jnp
from jax import lax
from jax.experimental import pallas as pl
from jax.experimental.pallas import tpu as pltpu
from jax.sharding import PartitionSpec as P

softening = 0.001
LANES = 128
MESH = pl.DeviceIdType.MESH
ROWS = 16
CAP = 12


def correct(old_pos, old_vel, old_acc, old_jerk, new_acc, new_jerk, timestep):
    halfstep = 0.5 * timestep
    twelfth = timestep * timestep / 12.0
    new_vel = old_vel + halfstep * (old_acc + new_acc) + twelfth * (old_jerk - new_jerk)
    new_pos = old_pos + halfstep * (old_vel + new_vel) + twelfth * (old_acc - new_acc)
    return (new_pos, new_vel)


def split_moments(block):
    zero = jnp.zeros((1, block.shape[1]), jnp.float32)
    block = jnp.concatenate([block, zero], axis=0)
    rows = lax.broadcasted_iota(jnp.int32, block.shape, 0)
    weighted = block * jnp.where(rows < 6, block[6:7], 1.0)
    high = weighted.astype(jnp.bfloat16).astype(jnp.float32)
    rest = weighted - high
    middle = rest.astype(jnp.bfloat16).astype(jnp.float32)
    low = rest - middle
    return jnp.concatenate([high, middle, low, jnp.zeros_like(block)], axis=0).astype(jnp.bfloat16)


def below(value):
    return value - value.astype(jnp.bfloat16).astype(jnp.float32)


def weigh_block(srcs, block, tb, moments, waccs, baccs):
    width = srcs.shape[2]
    moments[0:32, :] = split_moments(srcs[block])
    for tile in range(width // 256):
        at = tile * 256
        for unit in range(2):
            pltpu.matmul_push_rhs(
                moments[:, at : at + 256], staging_register=tile % 2, mxu_index=unit, transpose=True
            )
        source = [
            [
                jnp.broadcast_to(srcs[block, k : k + 1, at + h * LANES : at + (h + 1) * LANES], (ROWS, LANES))
                for k in range(6)
            ]
            for h in range(2)
        ]
        for part in range(len(waccs)):
            rows = pl.ds(part * ROWS, ROWS)
            target = [tb[k, rows, :] for k in range(6)]
            weights, bends = [], []
            for h in range(2):
                dx, dy, dz, ux, uy, uz = [source[h][k] - target[k] for k in range(6)]
                radius_sq = (dx * dx + dy * dy) + (dz * dz + softening)
                inverse = lax.rsqrt(radius_sq)
                inverse_sq = inverse * inverse
                weight = inverse * inverse_sq
                closing = (dx * ux + dy * uy) + dz * uz
                weights.append(weight)
                bends.append((weight * inverse_sq) * closing)
            weight = jnp.concatenate(weights, axis=1)
            bend = jnp.concatenate(bends, axis=1)
            fresh = tile % 2 if part < 2 else None
            pltpu.matmul_acc_lhs(waccs[part], weight, load_staged_rhs=fresh)
            pltpu.matmul_acc_lhs(baccs[part], bend)
            pltpu.matmul_acc_lhs(waccs[part], below(weight))
            pltpu.matmul_acc_lhs(baccs[part], below(bend))


def spread_targets(targets, tb):
    for b, tile in enumerate(targets):
        full = jnp.concatenate([tile, jnp.zeros((2, LANES), jnp.float32)], axis=0)
        columns = jnp.concatenate([full] * (LANES // 8), axis=0).T
        for k in range(6):
            tb[k, b * LANES : (b + 1) * LANES, :] = jnp.broadcast_to(columns[:, k : k + 1], (LANES, LANES))


def folded(accs, target):
    turned = jnp.concatenate([pltpu.matmul_pop(acc)[:, 0:LANES] for acc in accs], axis=0).T
    moment = turned[0:8] + turned[8:16] + turned[16:24]
    return moment[0:6] - target * moment[6:7]


def take_lanes(tile, index):
    return jnp.take_along_axis(tile, index, axis=1, mode="promise_in_bounds")


def turn(rows_of):
    return jnp.concatenate([rows_of] * (LANES // rows_of.shape[0]), axis=0).T


def slot_stars(ids, col, cols_n, stars, blocks):
    groups, size = ids.shape
    each = LANES // groups
    turned = turn(ids[...].astype(jnp.float32)).astype(jnp.int32)
    here = jnp.bitwise_and(lax.shift_right_arithmetic(turned, stars.bit_length() - 1), cols_n - 1) == col
    count = jnp.where(here, 1.0, 0.0)
    sub = lax.broadcasted_iota(jnp.int32, (8, LANES), 0)
    before = jnp.zeros((1, LANES), jnp.float32)
    ranks = []
    for i in range(size // 8):
        run = count[i * 8 : (i + 1) * 8]
        for step in (1, 2, 4):
            run = run + jnp.where(sub >= step, pltpu.roll(run, step, 0), 0.0)
        ranks.append(run + before - count[i * 8 : (i + 1) * 8])
        before = before + run[7:8]
    rank = jnp.where(here, jnp.concatenate(ranks, axis=0), -1.0)
    lane = lax.broadcasted_iota(jnp.int32, (1, LANES), 1)
    which = lax.shift_right_arithmetic(lane, groups.bit_length() - 1).astype(jnp.float32)
    found = []
    for b in range(blocks):
        hit = rank == which + float(b * each)
        found.append(jnp.sum(jnp.where(hit, turned + 1, 0), axis=0, keepdims=True) - 1)
    return found


def step_kernel(
    rows_n,
    cols_n,
    pos_h,
    vel_h,
    acc_h,
    jrk_h,
    mass_h,
    ela_h,
    ids_h,
    out_acc,
    out_jerk,
    out_flag,
    pos,
    vel,
    acc,
    jrk,
    mass,
    ela,
    ids,
    srcs,
    picked,
    near,
    part,
    parts,
    found,
    tb,
    moments,
    in_sems,
    send_sems,
    recv_sems,
    src_send,
    src_recv,
    *accs,
):
    row = lax.axis_index("row")
    col = lax.axis_index("col")
    stars = pos.shape[1]
    star_tiles = stars // LANES
    blocks = picked.shape[0]
    scale = 1.0 / (stars * rows_n * cols_n)
    waccs, baccs = accs[0::2], accs[1::2]

    loads = [
        pltpu.make_async_copy(src, dst, in_sems.at[i])
        for i, (src, dst) in enumerate(
            zip((ids_h, pos_h, vel_h, acc_h, jrk_h, mass_h, ela_h), (ids, pos, vel, acc, jrk, mass, ela))
        )
    ]
    for load in loads:
        load.start()

    barrier = pltpu.get_barrier_semaphore()
    for d in range(1, rows_n):
        pl.semaphore_signal(
            barrier, 1, device_id={"row": lax.rem(row + d, rows_n)}, device_id_type=MESH
        )
    for d in range(1, cols_n):
        pl.semaphore_signal(
            barrier, 1, device_id={"col": lax.rem(col + d, cols_n)}, device_id_type=MESH
        )

    loads[0].wait()
    slots = slot_stars(ids, col, cols_n, stars, blocks)
    for load in loads[1:]:
        load.wait()

    t = ela[...]
    p, v, a, j = pos[...], vel[...], acc[...], jrk[...]
    moved_pos = p + t * (v + t * (0.5 * a + t * j / 6.0))
    moved_vel = v + t * (a + 0.5 * t * j)
    own = jnp.concatenate([moved_pos, moved_vel, mass[...]], axis=0)
    srcs[0] = own
    padded = jnp.concatenate([own, jnp.zeros((1, stars), jnp.float32)], axis=0)

    first = (row * cols_n + col) * stars
    mine = []
    for b in range(blocks):
        local = jnp.broadcast_to(slots[b], (8, LANES)) - first
        lane = jnp.bitwise_and(local, LANES - 1)
        tile = jnp.zeros((8, LANES), jnp.float32)
        for s in range(star_tiles):
            held = jnp.logical_and(local >= s * LANES, local < (s + 1) * LANES)
            tile = jnp.where(held, take_lanes(padded[:, s * LANES : (s + 1) * LANES], lane), tile)
        mine.append(tile[0:6])
        picked[b] = tile[0:6]

    pl.semaphore_wait(barrier, rows_n - 1 + cols_n - 1)

    def send(src, dst, send_sem, recv_sem, axis, peer):
        pltpu.make_async_remote_copy(
            src_ref=src,
            dst_ref=dst,
            send_sem=send_sem,
            recv_sem=recv_sem,
            device_id={axis: peer},
            device_id_type=MESH,
        ).start()

    def whole(ref, send_sem, recv_sem):
        return pltpu.make_async_remote_copy(
            src_ref=ref,
            dst_ref=ref,
            send_sem=send_sem,
            recv_sem=recv_sem,
            device_id={"row": row},
            device_id_type=MESH,
        )

    for d in range(1, rows_n):
        peer = lax.rem(row + d, rows_n)
        send(picked, near.at[d - 1], send_sems.at[0], recv_sems.at[0], "row", peer)
    order = sorted(range(1, cols_n), key=lambda d: min(d, cols_n - d))
    for i, d in enumerate(order):
        peer = lax.rem(col + d, cols_n)
        send(srcs.at[0], srcs.at[i + 1], src_send.at[0], src_recv.at[i], "col", peer)

    sublane = lax.broadcasted_iota(jnp.int32, (8, LANES), 0)
    lane_f = lax.broadcasted_iota(jnp.int32, (8, LANES), 1).astype(jnp.float32)
    for k in range(stars // 8):
        star = first + k * 8 + sublane
        at = jnp.full((8, LANES), -1.0, jnp.float32)
        for b in range(blocks):
            at = jnp.where(jnp.broadcast_to(slots[b], (8, LANES)) == star, lane_f + float(b * LANES), at)
        found[k * 8 : (k + 1) * 8, :] = at
    spots = [
        jnp.max(found[s * LANES : (s + 1) * LANES, :].T, axis=0, keepdims=True).astype(jnp.int32)
        for s in range(star_tiles)
    ]
    moments[32:256, :] = jnp.zeros((224, stars), jnp.bfloat16)
    for unit_acc in accs:
        pltpu.matmul_pop(unit_acc)

    whole(near, send_sems.at[0], recv_sems.at[0]).wait_recv()
    targets = []
    for b in range(blocks):
        total = mine[b]
        for d in range(rows_n - 1):
            total = total + near[d, b]
        targets.append(total)
    spread_targets(targets, tb)

    def advance(i, carry):
        @pl.when(i > 0)
        def _():
            whole(srcs.at[0], src_send.at[0], src_recv.at[i - 1]).wait_recv()

        weigh_block(srcs, i, tb, moments, waccs, baccs)
        return carry

    lax.fori_loop(0, cols_n, advance, 0)

    each = LANES // ROWS
    summed = []
    for b in range(blocks):
        direct = folded(waccs[b * each : (b + 1) * each], targets[b])
        bent = folded(baccs[b * each : (b + 1) * each], targets[b])
        summed.append(jnp.concatenate([direct[0:3], direct[3:6] - 3.0 * bent[0:3]], axis=0))
        part[b] = summed[b]
    for d in range(1, rows_n):
        peer = lax.rem(row + d, rows_n)
        send(part, parts.at[d - 1], send_sems.at[1], recv_sems.at[1], "row", peer)
    whole(parts, send_sems.at[1], recv_sems.at[1]).wait_recv()
    forces = []
    for b in range(blocks):
        total = summed[b]
        for d in range(rows_n - 1):
            total = total + parts[d, b]
        forces.append(jnp.concatenate([total * scale, jnp.zeros((2, LANES), jnp.float32)], axis=0))

    for s in range(star_tiles):
        spot = jnp.broadcast_to(spots[s], (8, LANES))
        lane = jnp.bitwise_and(spot, LANES - 1)
        out = jnp.zeros((8, LANES), jnp.float32)
        for b in range(blocks):
            held = jnp.logical_and(spot >= b * LANES, spot < (b + 1) * LANES)
            out = jnp.where(held, take_lanes(forces[b], lane), out)
        lanes = slice(s * LANES, (s + 1) * LANES)
        out_acc[:, lanes] = out[0:3]
        out_jerk[:, lanes] = out[3:6]
        out_flag[:, lanes] = jnp.where(spot[0:3] >= 0, 1.0, 0.0)

    whole(near, send_sems.at[0], recv_sems.at[0]).wait_send()
    whole(srcs.at[pl.ds(1, cols_n - 1)], src_send.at[0], src_recv.at[0]).wait_send()
    whole(parts, send_sems.at[1], recv_sems.at[1]).wait_send()


def on_device(rows_n, cols_n, cap, positions, velocities, accels, jerks, masses, elapsed, active_star):
    stars = positions.shape[1]
    groups = rows_n
    size = active_star.shape[0] // groups
    blocks = cap * groups // LANES
    units = blocks * LANES // ROWS
    f32 = jnp.float32
    tiles = (blocks, 6, LANES)

    def kernel(*refs):
        accs = [pltpu.ACC((i // 2) % 2)((ROWS, 256), f32) for i in range(2 * units)]
        pl.run_scoped(functools.partial(step_kernel, rows_n, cols_n, *refs), *accs)

    shape = jax.ShapeDtypeStruct((3, stars), f32)
    new_acc, new_jerk, flag = pl.pallas_call(
        kernel,
        out_shape=(shape, shape, shape),
        in_specs=[pl.BlockSpec(memory_space=pltpu.HBM)] * 7,
        out_specs=(pl.BlockSpec(memory_space=pltpu.VMEM),) * 3,
        scratch_shapes=[
            pltpu.VMEM((3, stars), f32),
            pltpu.VMEM((3, stars), f32),
            pltpu.VMEM((3, stars), f32),
            pltpu.VMEM((3, stars), f32),
            pltpu.VMEM((1, stars), f32),
            pltpu.VMEM((1, stars), f32),
            pltpu.VMEM((groups, size), jnp.int32),
            pltpu.VMEM((cols_n, 7, stars), f32),
            pltpu.VMEM(tiles, f32),
            pltpu.VMEM((rows_n - 1,) + tiles, f32),
            pltpu.VMEM(tiles, f32),
            pltpu.VMEM((rows_n - 1,) + tiles, f32),
            pltpu.VMEM((stars, LANES), f32),
            pltpu.VMEM((6, blocks * LANES, LANES), f32),
            pltpu.VMEM((256, stars), jnp.bfloat16),
            pltpu.SemaphoreType.DMA((7,)),
            pltpu.SemaphoreType.DMA((2,)),
            pltpu.SemaphoreType.DMA((2,)),
            pltpu.SemaphoreType.DMA((1,)),
            pltpu.SemaphoreType.DMA((cols_n - 1,)),
        ],
        compiler_params=pltpu.CompilerParams(
            collective_id=0, has_side_effects=True
        ),
        name="block_step",
    )(
        positions,
        velocities,
        accels,
        jerks,
        masses[None, :],
        elapsed[None, :],
        active_star.reshape(groups, size),
    )
    active = flag > 0.5
    new_pos, new_vel = correct(
        positions, velocities, accels, jerks, new_acc, new_jerk, elapsed[None, :]
    )
    return (
        jnp.where(active, new_pos, positions),
        jnp.where(active, new_vel, velocities),
        jnp.where(active, new_acc, accels),
        jnp.where(active, new_jerk, jerks),
    )


def solution(mesh):
    split = P(None, ("row", "col"))
    flat = P(("row", "col"))
    return jax.shard_map(
        functools.partial(on_device, mesh.shape["row"], mesh.shape["col"], CAP),
        mesh=mesh,
        in_specs=(split, split, split, split, flat, flat, P()),
        out_specs=(split, split, split, split),
        check_vma=False,
    )
```

time: 63.6 us -> 49.1 us (0.77)
  Pallas kernels: 59.6 us -> 45.5 us
    pallas_call x1, Pallas kernels: 59.6 us -> 45.5 us  [on_device(): pl.pallas_call(kernel, out_shape=(shape, shape, shape), in_specs=[pl.Bloc...]
    select_n x0 -> x1, other arithmetic: none -> 1.33 us  [on_device(): jnp.where(active, new_jerk, jerks)]
    select_n x1, other arithmetic: 1.42 us -> 0.62 us  [on_device(): jnp.where(active, new_vel, velocities)]
    gt x1 -> x0, other arithmetic: 0.74 us -> none  [on_device(): active = landed[6:7] > 0.5]
where the time goes in v2:
time: 49.1 us; the launch traced here: 48.9 us
  Pallas kernels  45.5 us (93%)
  other arithmetic  1.96 us (4%)
  between operations  0.72 us (1%)
  local copies, waits for them, and re-layouts  0.71 us (1%)
    pallas_call x1, Pallas kernels, on_device(): pl.pallas_call(kernel, out_shape=(shape, shape, shape), in_specs=[pl.Bloc...  45.5 us
    select_n x1, other arithmetic, on_device(): jnp.where(active, new_jerk, jerks)  1.33 us

profile of v2, /device:TPU:1, one launch (start us, length us, event | category | flops | bytes accessed | tf_op | source)
XLA Modules:
  0.0 48.9 jit_solution(1334666826753929591)
XLA Ops:
  0.6 0.0 copy-start.6
  0.6 0.7 %copy-done.6 = f32[512]{0:T(512)S(1)} copy-done((f32[512]{0:T(512)S(1)}, f32[512]{0:T(512)}, u32[]{:S(2)}) %copy-start.6) | copy-done | bytes 2072
  1.3 0.0 copy-start
  1.3 45.5 %block_step.1 = (f32[3,512]{1,0:T(4,128)}, f32[3,512]{1,0:T(4,128)}, f32[3,512]{1,0:T(4,128)}) custom-call(f32[3,512]{1,0:T(4,128)} %refs_0_.1, f32[3,512]{1,0:T(4,128)} %refs_1_.1, f32[3,512]{1,0:T(4,128)} %refs_2_.1, f32[3,512]{1,0:T(4,128)} %refs_3_.1, f32[1,512]{1,0:T(1,128)} %bitcast.5, f32[1,512]{1,0:T(1,128)} %bitcast.4, s32[32,128]{1,0:T(8,128)} %bitcast.3), custom_call_target="tpu_custom_call" | custom-call | tf_op jit(solution)/shard_map/block_step/pallas_call | solution.py:327
  46.8 0.0 copy-start.5
  46.8 0.0 copy-done
  46.8 0.0 copy-start.1
  46.8 0.0 copy-start.2
  46.8 0.0 copy-start.3
  46.9 0.0 copy-start.4
  46.9 1.3 %fusion.1 = (f32[3,512]{1,0:T(4,128)}, pred[3,512]{1,0:T(4,128)(4,1)S(1)}) fusion(f32[3,512]{1,0:T(4,128)} %get-tuple-element.9, f32[3,512]{1,0:T(4,128)S(1)} %copy-done, f32[3,512]{1,0:T(4,128)} %get-tuple-element.7), kind=kLoop, calls=%fused_computation.6 | loop fusion | flops 3072 | bytes 26112 | tf_op jit(solution)/shard_map/jit(_where)/select_n | solution.py:375
  48.2 0.0 copy-done.5
  48.2 0.0 copy-done.1
  48.2 0.0 copy-done.2
  48.2 0.0 copy-done.3
  48.2 0.0 copy-done.4
  48.2 0.6 %fusion = (f32[3,512]{1,0:T(4,128)}, f32[3,512]{1,0:T(4,128)}, f32[3,512]{1,0:T(4,128)}) fusion(pred[3,512]{1,0:T(4,128)(4,1)S(1)} %get-tuple-element.11, f32[3,512]{1,0:T(4,128)S(1)} %copy-done.3, f32[3,512]{1,0:T(4,128)S(1)} %copy-done, f32[3,512]{1,0:T(4,128)S(1)} %copy-done.1, f32[512]{0:T(512)S(1)} %get-tuple-element.16, f32[3,512]{1,0:T(4,128)S(1)} %copy-done.4, ...), kind=kLoop, calls=%fused_computation.3 | loop fusion | flops 23040 | bytes 60928 | tf_op jit(solution)/shard_map/jit(_where)/select_n | solution.py:373
  (1 shorter events, 0.0 us)
Async XLA Ops:
  0.6 0.7 %copy-start.6 = (f32[512]{0:T(512)S(1)}, f32[512]{0:T(512)}, u32[]{:S(2)}) copy-start(f32[512]{0:T(512)} %param.12) | copy-start | bytes 6148
  1.3 45.5 %copy-start = (f32[3,512]{1,0:T(4,128)S(1)}, f32[3,512]{1,0:T(4,128)}, u32[]{:S(2)}) copy-start(f32[3,512]{1,0:T(4,128)} %refs_3_.1) | copy-start | bytes 18436
  46.8 1.4 %copy-start.5 = (f32[3,512]{1,0:T(4,128)S(1)}, f32[3,512]{1,0:T(4,128)}, u32[]{:S(2)}) copy-start(f32[3,512]{1,0:T(4,128)} %get-tuple-element.8) | copy-start | bytes 18436
  46.8 1.4 %copy-start.1 = (f32[3,512]{1,0:T(4,128)S(1)}, f32[3,512]{1,0:T(4,128)}, u32[]{:S(2)}) copy-start(f32[3,512]{1,0:T(4,128)} %get-tuple-element.9) | copy-start | bytes 18436
  46.8 1.4 %copy-start.2 = (f32[3,512]{1,0:T(4,128)S(1)}, f32[3,512]{1,0:T(4,128)}, u32[]{:S(2)}) copy-start(f32[3,512]{1,0:T(4,128)} %refs_0_.1) | copy-start | bytes 18436
  46.8 1.4 %copy-start.3 = (f32[3,512]{1,0:T(4,128)S(1)}, f32[3,512]{1,0:T(4,128)}, u32[]{:S(2)}) copy-start(f32[3,512]{1,0:T(4,128)} %refs_1_.1) | copy-start | bytes 18436
  46.9 1.4 %copy-start.4 = (f32[3,512]{1,0:T(4,128)S(1)}, f32[3,512]{1,0:T(4,128)}, u32[]{:S(2)}) copy-start(f32[3,512]{1,0:T(4,128)} %refs_2_.1) | copy-start | bytes 18436

commit v3 on v2

--- a/solution.py
+++ b/solution.py
@@ -133,9 +133,7 @@
     mass_h,
     ela_h,
     ids_h,
-    out_acc,
-    out_jerk,
-    out_flag,
+    out,
     pos,
     vel,
     acc,
@@ -156,6 +154,7 @@
     recv_sems,
     src_send,
     src_recv,
+    told,
     *accs,
 ):
     row = lax.axis_index("row")
@@ -176,13 +175,19 @@
         load.start()
 
     barrier = pltpu.get_barrier_semaphore()
-    for d in range(1, rows_n):
+    core = lax.rem(row, 2)
+    mate = row + 1 - 2 * core
+    pl.semaphore_signal(barrier, 1, device_id={"row": mate}, device_id_type=MESH)
+    for d in range(1, rows_n // 2):
         pl.semaphore_signal(
-            barrier, 1, device_id={"row": lax.rem(row + d, rows_n)}, device_id_type=MESH
+            barrier, 1, device_id={"row": lax.rem(row - core + 2 * d, rows_n)}, device_id_type=MESH
         )
     for d in range(1, cols_n):
         pl.semaphore_signal(
-            barrier, 1, device_id={"col": lax.rem(col + d, cols_n)}, device_id_type=MESH
+            barrier,
+            1,
+            device_id={"row": row - core + 1, "col": lax.rem(col + d, cols_n)},
+            device_id_type=MESH,
         )
 
     loads[0].wait()
@@ -210,7 +215,17 @@
         mine.append(tile[0:6])
         picked[b] = tile[0:6]
 
-    pl.semaphore_wait(barrier, rows_n - 1 + cols_n - 1)
+    def hear(listener, count):
+        @pl.when(core == listener)
+        def _():
+            pl.semaphore_wait(barrier, count)
+            pl.semaphore_signal(told, 1, device_id={"row": mate}, device_id_type=MESH)
+
+        @pl.when(core != listener)
+        def _():
+            pl.semaphore_wait(told, 1)
+
+    hear(0, rows_n - 1)
 
     def send(src, dst, send_sem, recv_sem, axis, peer):
         pltpu.make_async_remote_copy(
@@ -235,6 +250,7 @@
     for d in range(1, rows_n):
         peer = lax.rem(row + d, rows_n)
         send(picked, near.at[d - 1], send_sems.at[0], recv_sems.at[0], "row", peer)
+    hear(1, 2 * cols_n - 1)
     order = sorted(range(1, cols_n), key=lambda d: min(d, cols_n - d))
     for i, d in enumerate(order):
         peer = lax.rem(col + d, cols_n)
@@ -296,14 +312,20 @@
     for s in range(star_tiles):
         spot = jnp.broadcast_to(spots[s], (8, LANES))
         lane = jnp.bitwise_and(spot, LANES - 1)
-        out = jnp.zeros((8, LANES), jnp.float32)
+        place = jnp.zeros((8, LANES), jnp.float32)
         for b in range(blocks):
             held = jnp.logical_and(spot >= b * LANES, spot < (b + 1) * LANES)
-            out = jnp.where(held, take_lanes(forces[b], lane), out)
+            place = jnp.where(held, take_lanes(forces[b], lane), place)
         lanes = slice(s * LANES, (s + 1) * LANES)
-        out_acc[:, lanes] = out[0:3]
-        out_jerk[:, lanes] = out[3:6]
-        out_flag[:, lanes] = jnp.where(spot[0:3] >= 0, 1.0, 0.0)
+        active = spot[0:3] >= 0
+        new_acc, new_jerk = place[0:3], place[3:6]
+        new_pos, new_vel = correct(
+            pos[:, lanes], vel[:, lanes], acc[:, lanes], jrk[:, lanes], new_acc, new_jerk, ela[:, lanes]
+        )
+        out[0:3, lanes] = jnp.where(active, new_pos, pos[:, lanes])
+        out[4:7, lanes] = jnp.where(active, new_vel, vel[:, lanes])
+        out[8:11, lanes] = jnp.where(active, new_acc, acc[:, lanes])
+        out[12:15, lanes] = jnp.where(active, new_jerk, jrk[:, lanes])
 
     whole(near, send_sems.at[0], recv_sems.at[0]).wait_send()
     whole(srcs.at[pl.ds(1, cols_n - 1)], src_send.at[0], src_recv.at[0]).wait_send()
@@ -323,12 +345,11 @@
         accs = [pltpu.ACC((i // 2) % 2)((ROWS, 256), f32) for i in range(2 * units)]
         pl.run_scoped(functools.partial(step_kernel, rows_n, cols_n, *refs), *accs)
 
-    shape = jax.ShapeDtypeStruct((3, stars), f32)
-    new_acc, new_jerk, flag = pl.pallas_call(
+    merged = pl.pallas_call(
         kernel,
-        out_shape=(shape, shape, shape),
+        out_shape=jax.ShapeDtypeStruct((16, stars), f32),
         in_specs=[pl.BlockSpec(memory_space=pltpu.HBM)] * 7,
-        out_specs=(pl.BlockSpec(memory_space=pltpu.VMEM),) * 3,
+        out_specs=pl.BlockSpec(memory_space=pltpu.VMEM),
         scratch_shapes=[
             pltpu.VMEM((3, stars), f32),
             pltpu.VMEM((3, stars), f32),
@@ -350,6 +371,7 @@
             pltpu.SemaphoreType.DMA((2,)),
             pltpu.SemaphoreType.DMA((1,)),
             pltpu.SemaphoreType.DMA((cols_n - 1,)),
+            pltpu.SemaphoreType.REGULAR,
         ],
         compiler_params=pltpu.CompilerParams(
             collective_id=0, has_side_effects=True
@@ -364,16 +386,7 @@
         elapsed[None, :],
         active_star.reshape(groups, size),
     )
-    active = flag > 0.5
-    new_pos, new_vel = correct(
-        positions, velocities, accels, jerks, new_acc, new_jerk, elapsed[None, :]
-    )
-    return (
-        jnp.where(active, new_pos, positions),
-        jnp.where(active, new_vel, velocities),
-        jnp.where(active, new_acc, accels),
-        jnp.where(active, new_jerk, jerks),
-    )
+    return tuple(merged[4 * i : 4 * i + 3] for i in range(4))
 
 
 def solution(mesh):

time: 49.1 us -> 43.6 us (0.89)
  Pallas kernels: 45.5 us -> 41.3 us
  other arithmetic: 1.96 us -> 0 us
  local copies, waits for them, and re-layouts: 0.71 us -> 1.41 us
    pallas_call x1, Pallas kernels: 45.5 us -> 41.3 us  [on_device(): pl.pallas_call(kernel, out_shape=jax.ShapeDtypeStruct((16, stars), f32),...]
    select_n x2 -> x0, other arithmetic: 1.96 us -> none  [the longest x1 1.33 us: on_device(): jnp.where(active, new_jerk, jerks)]
    slice x0 -> x1, local copies, waits for them, and re-layouts: none -> 1.41 us  [on_device(): return tuple((merged[4 * i:4 * i + 3] for i in range(4)))]
    unnamed x14 -> x0, local copies, waits for them, and re-layouts: 0.71 us -> none
where the time goes in v3:
time: 43.6 us; the launch traced here: 43.4 us
  Pallas kernels  41.3 us (95%)
  local copies, waits for them, and re-layouts  1.41 us (3%)
  between operations  0.64 us (1%)
    pallas_call x1, Pallas kernels, on_device(): pl.pallas_call(kernel, out_shape=jax.ShapeDtypeStruct((16, stars), f32),...  41.3 us
    slice x1, local copies, waits for them, and re-layouts, on_device(): return tuple((merged[4 * i:4 * i + 3] for i in range(4)))  1.41 us

profile of v3, /device:TPU:1, one launch (start us, length us, event | category | flops | bytes accessed | tf_op | source)
XLA Modules:
  0.0 43.4 jit_solution(2273074009680136148)
XLA Ops:
  0.6 41.3 %block_step.1 = f32[16,512]{1,0:T(8,128)} custom-call(f32[3,512]{1,0:T(4,128)} %refs_0_.1, f32[3,512]{1,0:T(4,128)} %refs_1_.1, f32[3,512]{1,0:T(4,128)} %refs_2_.1, f32[3,512]{1,0:T(4,128)} %refs_3_.1, f32[1,512]{1,0:T(1,128)} %bitcast.4, f32[1,512]{1,0:T(1,128)} %bitcast.5, s32[32,128]{1,0:T(8,128)} %bitcast.3), custom_call_target="tpu_custom_call" | custom-call | tf_op jit(solution)/shard_map/block_step/pallas_call | solution.py:348
  41.9 1.4 %fusion = (f32[3,512]{1,0:T(4,128)}, f32[3,512]{1,0:T(4,128)}, f32[3,512]{1,0:T(4,128)}, f32[3,512]{1,0:T(4,128)}) fusion(f32[16,512]{1,0:T(8,128)} %block_step.1), kind=kLoop, calls=%fused_computation | loop fusion | bytes 49152 | tf_op jit(solution)/shard_map/slice | solution.py:389

commit v4 on v3

--- a/solution.py
+++ b/solution.py
@@ -155,6 +155,7 @@
     src_send,
     src_recv,
     told,
+    beyond,
     *accs,
 ):
     row = lax.axis_index("row")
@@ -177,17 +178,19 @@
     barrier = pltpu.get_barrier_semaphore()
     core = lax.rem(row, 2)
     mate = row + 1 - 2 * core
+    reach = cols_n // 4
+    near_by = [s * d for d in range(1, reach + 1) for s in (1, -1)]
     pl.semaphore_signal(barrier, 1, device_id={"row": mate}, device_id_type=MESH)
+    for d in reversed(near_by):
+        pl.semaphore_signal(
+            barrier,
+            1,
+            device_id={"row": row - core + 1, "col": lax.rem(col + d + cols_n, cols_n)},
+            device_id_type=MESH,
+        )
     for d in range(1, rows_n // 2):
         pl.semaphore_signal(
             barrier, 1, device_id={"row": lax.rem(row - core + 2 * d, rows_n)}, device_id_type=MESH
-        )
-    for d in range(1, cols_n):
-        pl.semaphore_signal(
-            barrier,
-            1,
-            device_id={"row": row - core + 1, "col": lax.rem(col + d, cols_n)},
-            device_id_type=MESH,
         )
 
     loads[0].wait()
@@ -215,11 +218,14 @@
         mine.append(tile[0:6])
         picked[b] = tile[0:6]
 
+    def tell_mate():
+        pl.semaphore_signal(told, 1, device_id={"row": mate}, device_id_type=MESH)
+
     def hear(listener, count):
         @pl.when(core == listener)
         def _():
             pl.semaphore_wait(barrier, count)
-            pl.semaphore_signal(told, 1, device_id={"row": mate}, device_id_type=MESH)
+            tell_mate()
 
         @pl.when(core != listener)
         def _():
@@ -250,11 +256,43 @@
     for d in range(1, rows_n):
         peer = lax.rem(row + d, rows_n)
         send(picked, near.at[d - 1], send_sems.at[0], recv_sems.at[0], "row", peer)
-    hear(1, 2 * cols_n - 1)
-    order = sorted(range(1, cols_n), key=lambda d: min(d, cols_n - d))
-    for i, d in enumerate(order):
-        peer = lax.rem(col + d, cols_n)
-        send(srcs.at[0], srcs.at[i + 1], src_send.at[0], src_recv.at[i], "col", peer)
+    far_off = [s * d for d in range(reach + 1, cols_n // 2 + 1) for s in (1, -1)][:-1]
+
+    def share():
+        def give(d):
+            slot = 2 * abs(d) - (1 if d > 0 else 0)
+            peer = lax.rem(col + d + cols_n, cols_n)
+            send(srcs.at[0], srcs.at[slot], src_send.at[0], src_recv.at[slot - 1], "col", peer)
+
+        hear(1, 2 * len(near_by) + 1)
+
+        @pl.when(core == 1)
+        def _():
+            for side, d in enumerate((reach, -reach)):
+                pl.semaphore_signal(
+                    beyond.at[side],
+                    1,
+                    device_id={"col": lax.rem(col + d + cols_n, cols_n)},
+                    device_id_type=MESH,
+                )
+
+        for d in near_by:
+            give(d)
+
+        @pl.when(core == 1)
+        def _():
+            pl.semaphore_wait(beyond.at[0], 1)
+            pl.semaphore_wait(beyond.at[1], 1)
+            tell_mate()
+
+        @pl.when(core != 1)
+        def _():
+            pl.semaphore_wait(told, 1)
+
+        for d in far_off:
+            give(d)
+
+    share()
 
     sublane = lax.broadcasted_iota(jnp.int32, (8, LANES), 0)
     lane_f = lax.broadcasted_iota(jnp.int32, (8, LANES), 1).astype(jnp.float32)
@@ -281,15 +319,14 @@
         targets.append(total)
     spread_targets(targets, tb)
 
+    weigh_block(srcs, 0, tb, moments, waccs, baccs)
+
     def advance(i, carry):
-        @pl.when(i > 0)
-        def _():
-            whole(srcs.at[0], src_send.at[0], src_recv.at[i - 1]).wait_recv()
-
+        whole(srcs.at[0], src_send.at[0], src_recv.at[i - 1]).wait_recv()
         weigh_block(srcs, i, tb, moments, waccs, baccs)
         return carry
 
-    lax.fori_loop(0, cols_n, advance, 0)
+    lax.fori_loop(1, cols_n, advance, 0)
 
     each = LANES // ROWS
     summed = []
@@ -372,6 +409,7 @@
             pltpu.SemaphoreType.DMA((1,)),
             pltpu.SemaphoreType.DMA((cols_n - 1,)),
             pltpu.SemaphoreType.REGULAR,
+            pltpu.SemaphoreType.REGULAR((2,)),
         ],
         compiler_params=pltpu.CompilerParams(
             collective_id=0, has_side_effects=True

time: 43.6 us -> 42.9 us (0.984)
  Pallas kernels: 41.3 us -> 40.6 us
    pallas_call x1, Pallas kernels: 41.3 us -> 40.6 us  [on_device(): pl.pallas_call(kernel, out_shape=jax.ShapeDtypeStruct((16, stars), f32),...]
where the time goes in v4:
time: 42.9 us; the launch traced here: 42.7 us
  Pallas kernels  40.6 us (95%)
  local copies, waits for them, and re-layouts  1.41 us (3%)
  between operations  0.64 us (1%)
    pallas_call x1, Pallas kernels, on_device(): pl.pallas_call(kernel, out_shape=jax.ShapeDtypeStruct((16, stars), f32),...  40.6 us
    slice x1, local copies, waits for them, and re-layouts, on_device(): return tuple((merged[4 * i:4 * i + 3] for i in range(4)))  1.41 us

profile of v4, /device:TPU:1, one launch (start us, length us, event | category | flops | bytes accessed | tf_op | source)
XLA Modules:
  0.0 42.7 jit_solution(16554626274030452153)
XLA Ops:
  0.6 40.6 %block_step.1 = f32[16,512]{1,0:T(8,128)} custom-call(f32[3,512]{1,0:T(4,128)} %refs_0_.1, f32[3,512]{1,0:T(4,128)} %refs_1_.1, f32[3,512]{1,0:T(4,128)} %refs_2_.1, f32[3,512]{1,0:T(4,128)} %refs_3_.1, f32[1,512]{1,0:T(1,128)} %bitcast.4, f32[1,512]{1,0:T(1,128)} %bitcast.5, s32[32,128]{1,0:T(8,128)} %bitcast.3), custom_call_target="tpu_custom_call" | custom-call | tf_op jit(solution)/shard_map/block_step/pallas_call | solution.py:385
  41.3 1.4 %fusion = (f32[3,512]{1,0:T(4,128)}, f32[3,512]{1,0:T(4,128)}, f32[3,512]{1,0:T(4,128)}, f32[3,512]{1,0:T(4,128)}) fusion(f32[16,512]{1,0:T(8,128)} %block_step.1), kind=kLoop, calls=%fused_computation | loop fusion | bytes 49152 | tf_op jit(solution)/shard_map/slice | solution.py:427

commit v5 on v4

--- a/solution.py
+++ b/solution.py
@@ -384,7 +384,7 @@
 
     merged = pl.pallas_call(
         kernel,
-        out_shape=jax.ShapeDtypeStruct((16, stars), f32),
+        out_shape=pltpu.VMEM((16, stars), f32),
         in_specs=[pl.BlockSpec(memory_space=pltpu.HBM)] * 7,
         out_specs=pl.BlockSpec(memory_space=pltpu.VMEM),
         scratch_shapes=[

time: 42.9 us -> 41.4 us (0.965)
  local copies, waits for them, and re-layouts: 1.41 us -> 0.62 us
  Pallas kernels: 40.6 us -> 40 us
    slice x1, local copies, waits for them, and re-layouts: 1.41 us -> 0.62 us  [on_device(): return tuple((merged[4 * i:4 * i + 3] for i in range(4)))]
    pallas_call x1, Pallas kernels: 40.6 us -> 40 us  [on_device(): pl.pallas_call(kernel, out_shape=pltpu.VMEM((16, stars), f32), in_specs=[...]
where the time goes in v5:
time: 41.4 us; the launch traced here: 41.3 us
  Pallas kernels  40 us (97%)
  between operations  0.64 us (2%)
  local copies, waits for them, and re-layouts  0.62 us (1%)
    pallas_call x1, Pallas kernels, on_device(): pl.pallas_call(kernel, out_shape=pltpu.VMEM((16, stars), f32), in_specs=[...  40 us

profile of v5, /device:TPU:1, one launch (start us, length us, event | category | flops | bytes accessed | tf_op | source)
XLA Modules:
  0.0 41.3 jit_solution(9568164396011736860)
XLA Ops:
  0.6 40.0 %block_step.1 = f32[16,512]{1,0:T(8,128)S(1)} custom-call(f32[3,512]{1,0:T(4,128)} %refs_0_.1, f32[3,512]{1,0:T(4,128)} %refs_1_.1, f32[3,512]{1,0:T(4,128)} %refs_2_.1, f32[3,512]{1,0:T(4,128)} %refs_3_.1, f32[1,512]{1,0:T(1,128)} %bitcast.4, f32[1,512]{1,0:T(1,128)} %bitcast.5, s32[32,128]{1,0:T(8,128)} %bitcast.3), custom_call_target="tpu_custom_call" | custom-call | tf_op jit(solution)/shard_map/block_step/pallas_call | solution.py:385
  40.6 0.6 %fusion = (f32[3,512]{1,0:T(4,128)}, f32[3,512]{1,0:T(4,128)}, f32[3,512]{1,0:T(4,128)}, f32[3,512]{1,0:T(4,128)}) fusion(f32[16,512]{1,0:T(8,128)S(1)} %block_step.1), kind=kLoop, calls=%fused_computation | loop fusion | bytes 49152 | tf_op jit(solution)/shard_map/slice | solution.py:427

commit v6 on v5

--- a/solution.py
+++ b/solution.py
@@ -1,4 +1,5 @@
 import functools
+import math
 
 import jax
 import jax.numpy as jnp
@@ -23,8 +24,6 @@
 
 
 def split_moments(block):
-    zero = jnp.zeros((1, block.shape[1]), jnp.float32)
-    block = jnp.concatenate([block, zero], axis=0)
     rows = lax.broadcasted_iota(jnp.int32, block.shape, 0)
     weighted = block * jnp.where(rows < 6, block[6:7], 1.0)
     high = weighted.astype(jnp.bfloat16).astype(jnp.float32)
@@ -203,8 +202,8 @@
     moved_pos = p + t * (v + t * (0.5 * a + t * j / 6.0))
     moved_vel = v + t * (a + 0.5 * t * j)
     own = jnp.concatenate([moved_pos, moved_vel, mass[...]], axis=0)
-    srcs[0] = own
     padded = jnp.concatenate([own, jnp.zeros((1, stars), jnp.float32)], axis=0)
+    srcs[0] = padded
 
     first = (row * cols_n + col) * stars
     mine = []
@@ -253,9 +252,18 @@
             device_id_type=MESH,
         )
 
-    for d in range(1, rows_n):
-        peer = lax.rem(row + d, rows_n)
-        send(picked, near.at[d - 1], send_sems.at[0], recv_sems.at[0], "row", peer)
+    side = math.isqrt(rows_n // 2)
+    y, x = row // (2 * side), lax.rem(row // 2, side)
+    steps = sorted(
+        ((dy, dx, dc) for dy in range(side) for dx in range(side) for dc in range(2)),
+        key=lambda s: (s != (0, 0, 0), -min(s[0], side - s[0]) - min(s[1], side - s[1])),
+    )[1:]
+    peers = [
+        2 * (side * lax.rem(y + dy, side) + lax.rem(x + dx, side)) + lax.rem(core + dc, 2)
+        for dy, dx, dc in steps
+    ]
+    for n, peer in enumerate(peers):
+        send(picked, near.at[n], send_sems.at[0], recv_sems.at[0], "row", peer)
     far_off = [s * d for d in range(reach + 1, cols_n // 2 + 1) for s in (1, -1)][:-1]
 
     def share():
@@ -335,9 +343,8 @@
         bent = folded(baccs[b * each : (b + 1) * each], targets[b])
         summed.append(jnp.concatenate([direct[0:3], direct[3:6] - 3.0 * bent[0:3]], axis=0))
         part[b] = summed[b]
-    for d in range(1, rows_n):
-        peer = lax.rem(row + d, rows_n)
-        send(part, parts.at[d - 1], send_sems.at[1], recv_sems.at[1], "row", peer)
+    for n, peer in enumerate(peers):
+        send(part, parts.at[n], send_sems.at[1], recv_sems.at[1], "row", peer)
     whole(parts, send_sems.at[1], recv_sems.at[1]).wait_recv()
     forces = []
     for b in range(blocks):
@@ -395,7 +402,7 @@
             pltpu.VMEM((1, stars), f32),
             pltpu.VMEM((1, stars), f32),
             pltpu.VMEM((groups, size), jnp.int32),
-            pltpu.VMEM((cols_n, 7, stars), f32),
+            pltpu.VMEM((cols_n, 8, stars), f32),
             pltpu.VMEM(tiles, f32),
             pltpu.VMEM((rows_n - 1,) + tiles, f32),
             pltpu.VMEM(tiles, f32),

time: 41.4 us -> 41.4 us (level)
  no operation moved by 1% of the time
where the time goes in v6:
time: 41.4 us; the launch traced here: 41.2 us
  Pallas kernels  40 us (97%)
  between operations  0.64 us (2%)
  local copies, waits for them, and re-layouts  0.62 us (1%)
    pallas_call x1, Pallas kernels, on_device(): pl.pallas_call(kernel, out_shape=pltpu.VMEM((16, stars), f32), in_specs=[...  40 us

profile of v6, /device:TPU:1, one launch (start us, length us, event | category | flops | bytes accessed | tf_op | source)
XLA Modules:
  0.0 41.2 jit_solution(11729918569067194041)
XLA Ops:
  0.6 40.0 %block_step.1 = f32[16,512]{1,0:T(8,128)S(1)} custom-call(f32[3,512]{1,0:T(4,128)} %refs_0_.1, f32[3,512]{1,0:T(4,128)} %refs_1_.1, f32[3,512]{1,0:T(4,128)} %refs_2_.1, f32[3,512]{1,0:T(4,128)} %refs_3_.1, f32[1,512]{1,0:T(1,128)} %bitcast.4, f32[1,512]{1,0:T(1,128)} %bitcast.5, s32[32,128]{1,0:T(8,128)} %bitcast.3), custom_call_target="tpu_custom_call" | custom-call | tf_op jit(solution)/shard_map/block_step/pallas_call | solution.py:392
  40.6 0.6 %fusion = (f32[3,512]{1,0:T(4,128)}, f32[3,512]{1,0:T(4,128)}, f32[3,512]{1,0:T(4,128)}, f32[3,512]{1,0:T(4,128)}) fusion(f32[16,512]{1,0:T(8,128)S(1)} %block_step.1), kind=kLoop, calls=%fused_computation | loop fusion | bytes 49152 | tf_op jit(solution)/shard_map/slice | solution.py:434
